TPU v7x, 128 devices: a whole 4x4x4 slice. The times are simulated.
128 devices in a mesh: dp: 16 (over z, y), expert: 8 (over x, core).
Axes of the slice: x: 4, y: 4, z: 4, core: 2. Of those that a mesh axis runs over, the one named last changes fastest.
Arguments:
- tokens: bfloat16 [2048, 4096], P('dp'), may hold values from -6 to 6
- expert_ids: int32 [2048, 2], P('dp'), may hold values from 0 to 7, all different within a row; in each aligned block of 128 rows (0 to 127, 128 to 255, ...) at most 96 rows name the same one
- gate_weights: float32 [2048, 2], P('dp'), may hold values from 0.2 to 1
- live_counts: int32 [16], P('dp'), may hold values from 64 to 128, as said below
- w_gate: bfloat16 [8, 4096, 8192], P('expert', None, 'dp'), may hold values from -0.09375 to 0.09375
- w_up: bfloat16 [8, 4096, 8192], P('expert', None, 'dp'), may hold values from -0.09375 to 0.09375
- w_down: bfloat16 [8, 8192, 4096], P('expert', 'dp'), may hold values from -0.0625 to 0.0625
Outputs:
- mixed: bfloat16 [2048, 4096], P('dp')
- total_loads: int32 [8], replicated
Inputs may be any that keep to these rules, and one draw needn't show every extreme that they name: `expert_ids`: each token names two different experts. Among the tokens of one rank no expert is named more than 96 times, a bound that some block reaches in some ranks. Rank r's first live_counts[r] tokens are live, the rest are padding. Some rank has all 128 tokens live.
All inputs are finite; a program needn't handle non-finite values.
Results may differ from a plain program's by a relative error of at most 0.017.
Values may be sent and summed in bfloat16 or wider, within the bound.
No kernel may reach another device: no remote copies, remote signals or barrier semaphores. Data moves between devices by JAX's collectives and lax.ppermute only.
A program may use at most 128 MiB of HBM per device.

v0:
```python
import jax
import jax.numpy as jnp
from jax import lax
from jax.sharding import Mesh
from jax.sharding import PartitionSpec as P

DP = ("dp_0", "dp_1")


def split_up(shard, dim, size):
    before, after = (shard.shape[:dim], shard.shape[dim + 1 :])
    return jnp.moveaxis(shard.reshape(*before, size, -1, *after), dim, 0)


def sum_at_owner(shard, axis, dim):
    size = lax.axis_size(axis)
    tiles = lax.all_to_all(split_up(shard, dim, size), axis, 0, 0, tiled=True)
    return jnp.sum(tiles.astype(jnp.float32), axis=0)


def from_everyone(shard, axis):
    copies = jnp.broadcast_to(shard, (lax.axis_size(axis), *shard.shape))
    return lax.all_to_all(copies, axis, split_axis=0, concat_axis=0, tiled=True)


def laid_out(tiles, dim):
    dims = list(tiles.shape[1:])
    dims[dim] *= tiles.shape[0]
    return jnp.moveaxis(tiles, 0, dim).reshape(dims)


def gather_directly(shard, axis, dim):
    tiles = from_everyone(shard, axis)
    return laid_out(tiles, dim)


def over_axes(shard, axes):
    for axis in axes:
        shard = lax.psum(shard, axis)
    return shard


def plan_routes(expert_ids, live_total, n_experts, capacity):
    row_count = expert_ids.shape[0]
    is_live = jnp.arange(row_count, dtype=jnp.int32) < live_total
    flat_ids = expert_ids.reshape(-1)
    live_pairs = jnp.repeat(is_live, 2)
    one_hot = (
        (flat_ids[:, None] == jnp.arange(n_experts, dtype=jnp.int32)[None, :]) & live_pairs[:, None]
    ).astype(jnp.int32)
    earlier = jnp.cumsum(one_hot, axis=0) - one_hot
    slot_index = jnp.sum(earlier * one_hot, axis=1)
    targets = jnp.where(live_pairs, flat_ids * capacity + slot_index, -1)
    return (targets.reshape(row_count, 2), jnp.sum(one_hot, axis=0))


def dispatch_rows(tokens, targets, slots_all):
    wanted = targets.reshape(-1)[None, :] == jnp.arange(slots_all, dtype=jnp.int32)[:, None]
    wanted = jnp.any(wanted.reshape(slots_all, -1, 2), axis=2).astype(jnp.bfloat16)
    return jnp.dot(wanted, tokens, preferred_element_type=jnp.float32).astype(jnp.bfloat16)


def per_device(tokens, expert_ids, gate_weights, live_counts, w_gate, w_up, w_down):
    n_experts = lax.axis_size("expert")
    my_expert = lax.axis_index("expert")
    capacity = 3 * tokens.shape[0] // 4
    targets, expert_loads = plan_routes(expert_ids, live_counts[0], n_experts, capacity)
    local_slots = targets - my_expert * capacity
    outbound = dispatch_rows(tokens, local_slots, capacity)
    gathered = lax.all_gather(outbound, DP, axis=0, tiled=True)
    gate_matrix = w_gate[0]
    up_matrix = w_up[0]
    down_matrix = w_down[0]
    gate_act = jnp.dot(gathered, gate_matrix, preferred_element_type=jnp.float32)
    up_act = jnp.dot(gathered, up_matrix, preferred_element_type=jnp.float32)
    hidden = (jax.nn.silu(gate_act) * up_act).astype(jnp.bfloat16)
    summed = lax.psum_scatter(
        jnp.dot(hidden, down_matrix, preferred_element_type=jnp.float32).astype(jnp.bfloat16),
        DP,
        scatter_dimension=0,
        tiled=True,
    )
    is_mine = (local_slots >= 0) & (local_slots < capacity)
    pick_index = jnp.where(is_mine, local_slots, 0)
    selected = summed[pick_index].astype(jnp.float32)
    weights = jnp.where(is_mine, gate_weights, jnp.zeros_like(gate_weights))
    weighted = jnp.sum(weights[:, :, None] * selected, axis=1)
    share = sum_at_owner(weighted.astype(jnp.bfloat16), "expert", 0).astype(jnp.bfloat16)
    mixed = gather_directly(share, "expert", 0)
    total_loads = over_axes(expert_loads, DP)
    return (mixed, total_loads)


def solution(mesh):
    torus = Mesh(mesh.devices.reshape(4, 4, mesh.shape["expert"]), ("dp_0", "dp_1", "expert"))
    in_specs = (
        P(DP, None),
        P(DP, None),
        P(DP, None),
        P(DP),
        P("expert", None, DP),
        P("expert", None, DP),
        P("expert", DP, None),
    )
    out_specs = (P(DP, None), P())
    return jax.shard_map(
        per_device, mesh=torus, in_specs=in_specs, out_specs=out_specs, check_vma=False
    )
```

profile of v0, /device:TPU:2, one launch (start us, length us, event | category | flops | bytes accessed | tf_op | source)
XLA Modules:
  0.0 302.2 jit_solution(7526284278638504880)
XLA Ops:
  7.2 0.0 copy-start
  7.2 0.0 all-gather.2.cloned.1.call-start
  7.2 0.8 broadcast_multiply_fusion
  8.0 0.8 copy.17
  8.8 0.1 eq.43
  8.9 0.1 eq.39
  9.7 0.1 broadcast_in_dim.26
  9.8 0.1 broadcast_in_dim.27
  10.0 0.1 broadcast_in_dim.25
  10.1 0.1 and.20
  10.2 0.1 copy.19
  10.3 0.6 reduce-window.6
  10.9 0.2 slice_reduce_fusion
  11.2 0.1 convert_reduce_fusion
  11.3 0.1 reduce_sum.42
  11.5 0.8 copy.20
  12.3 0.1 fusion.15
  12.4 0.1 copy.21
  12.5 0.0 copy-done
  12.5 1.2 convolution_convert_fusion.1
  13.7 0.0 all-gather.2.cloned.1.call-update
  13.8 0.0 reduce-scatter.2.cloned.1.call-start
  13.8 92.4 %all-gather.2.cloned.1.call-done = bf16[1536,4096]{1,0:T(8,128)(2,1)} async-done(((bf16[96,4096]{1,0:T(8,128)(2,1)}), bf16[1536,4096]{1,0:T(8,128)(2,1)}) %all-gather.2.cloned.1.call-update) | async-done | bytes 12582928 | tf_op jit(solution)/shard_map/all_gather | solution.py:70
  106.2 12.0 %fusion.3 = f32[1536,512]{1,0:T(8,128)} fusion(bf16[1536,4096]{1,0:T(8,128)(2,1)} %all-gather.2.cloned.1.call-done, bf16[1,4096,512]{2,1,0:T(8,128)(2,1)} %param.11), kind=kOutput, calls=%fused_computation.6 | convolution fusion | flops 6442450944 | bytes 19922944 | tf_op jit(solution)/shard_map/dot_general | solution.py:74
  118.2 21.8 %convolution_convert_fusion = bf16[1536,4096]{1,0:T(8,128)(2,1)} fusion(bf16[1,512,4096]{2,1,0:T(8,128)(2,1)} %param.13, bf16[1536,4096]{1,0:T(8,128)(2,1)} %all-gather.2.cloned.1.call-done, bf16[1,4096,512]{2,1,0:T(8,128)(2,1)} %param.12, f32[1536,512]{1,0:T(8,128)} %fusion.3), kind=kOutput, calls=%fused_computation.1 | convolution fusion | flops 12895911936 | bytes 36700160 | tf_op jit(solution)/shard_map/dot_general | solution.py:78
  140.0 0.0 reduce-scatter.2.cloned.1.call-update
  140.1 0.1 reshape.55
  140.2 95.1 %reduce-scatter.2.cloned.1.call-done = bf16[96,4096]{1,0:T(8,128)(2,1)} async-done(((bf16[1536,4096]{1,0:T(8,128)(2,1)}), bf16[96,4096]{1,0:T(8,128)(2,1)}) %reduce-scatter.2.cloned.1.call-update) | async-done | bytes 786448 | tf_op jit(solution)/shard_map/reduce_scatter | solution.py:77
  235.3 5.1 %gather_fusion = bf16[256,4096]{1,0:T(8,128)(2,1)S(1)} fusion(bf16[96,4096]{1,0:T(8,128)(2,1)} %reduce-scatter.2.cloned.1.call-done, s32[1024]{0:T(1024)S(1)} %pad_clamp_fusion), kind=kCustom, calls=%fused_computation | custom fusion | bytes 4195328 | tf_op jit(solution)/shard_map/gather | solution.py:85
  240.4 4.0 %reshape.63 = f32[128,2,4096]{2,1,0:T(2,128)} reshape(bf16[256,4096]{1,0:T(8,128)(2,1)S(1)} %gather_fusion) | data formatting | bytes 6291456 | tf_op jit(solution)/shard_map/convert_element_type | solution.py:85
  244.4 8.7 %multiply_reduce_fusion = bf16[128,4096]{1,0:T(8,128)(2,1)S(1)} fusion(f32[128,2,4096]{2,1,0:T(2,128)} %reshape.63, f32[128,2]{1,0:T(8,128)S(1)} %get-tuple-element.4), kind=kLoop, calls=%fused_computation.8 | loop fusion | flops 1572864 | bytes 5243904 | tf_op jit(solution)/shard_map/reduce_sum | solution.py:87
  253.1 19.2 %all_to_all.10 = bf16[8,16,4096]{2,1,0:T(8,128)(2,1)S(1)} all-to-all(bf16[8,16,4096]{2,1,0:T(8,128)(2,1)S(1)} %bitcast.29), channel_id=1, replica_groups=mesh['dp_0'=4,'dp_1'=4,'expert'=8] {'expert'}, dimensions={0} | all-to-all | bytes 2097152 | tf_op jit(solution)/shard_map/all_to_all | solution.py:17
  272.3 0.1 reduce_sum.44
  272.4 1.1 broadcast_in_dim.31
  273.5 4.9 %all-to-all-start.1 = ((bf16[8,16,4096]{2,1,0:T(8,128)(2,1)}), bf16[8,16,4096]{2,1,0:T(8,128)(2,1)S(1)}, u32[]{:S(2)}, u32[]{:S(2)}) async-start(bf16[8,16,4096]{2,1,0:T(8,128)(2,1)} %broadcast_in_dim.31), calls=%async_computation.2 | async-start | bytes 2097152 | tf_op jit(solution)/shard_map/all_to_all | solution.py:23
  278.4 8.2 %psum.14 = s32[8]{0:T(128)S(1)} all-reduce(s32[8]{0:T(128)S(1)} %get-tuple-element.2), channel_id=1, replica_groups=mesh['dp_0'=4,'dp_1'=4,'expert'=8] {'dp_0'}, use_global_device_ids=true, to_apply=%region_8.9 | all-reduce | flops 8 | bytes 64 | tf_op jit(solution)/shard_map/psum | solution.py:39
  286.5 7.8 %psum.15 = s32[8]{0:T(128)} all-reduce(s32[8]{0:T(128)S(1)} %psum.14), channel_id=1, replica_groups=mesh['dp_0'=4,'dp_1'=4,'expert'=8] {'dp_1'}, use_global_device_ids=true, to_apply=%region_9.10 | all-reduce | flops 8 | bytes 64 | tf_op jit(solution)/shard_map/psum | solution.py:39
  294.4 0.0 all-to-all-done.1
  294.4 1.0 copy.25
  (8 shorter events, 0.1 us)
Async XLA Ops:
  7.2 5.3 %copy-start = (bf16[128,4096]{1,0:T(8,128)(2,1)S(1)}, bf16[128,4096]{1,0:T(8,128)(2,1)}, u32[]{:S(2)}) copy-start(bf16[128,4096]{1,0:T(8,128)(2,1)} %param.7) | copy-start | bytes 3145732
  7.2 99.0 %all-gather.2.cloned.1.call-start = ((), (), s32[]{:S(2)}) async-start(), calls=%async_computation.3 | async-start | bytes 13369344 | tf_op jit(solution)/shard_map/all_gather | solution.py:70
  13.8 221.5 %reduce-scatter.2.cloned.1.call-start = ((), (), s32[]{:S(2)}) async-start(), calls=%async_computation.4 | async-start | bytes 13369344 | tf_op jit(solution)/shard_map/reduce_scatter | solution.py:77
  273.5 20.9 %all-to-all-start.1 = ((bf16[8,16,4096]{2,1,0:T(8,128)(2,1)}), bf16[8,16,4096]{2,1,0:T(8,128)(2,1)S(1)}, u32[]{:S(2)}, u32[]{:S(2)}) async-start(bf16[8,16,4096]{2,1,0:T(8,128)(2,1)} %broadcast_in_dim.31), calls=%async_computation.2 | async-start | bytes 2097152 | tf_op jit(solution)/shard_map/all_to_all | solution.py:23
Sparse Core Ops, SparseCore 0:
  13.9 92.2 all-gather.1
  140.1 95.1 reduce-scatter.1
where the time goes:
time: 303 us; the launch traced here: 302 us
  waiting for transfers between devices  188 us (62%)
  blocking collectives  35.2 us (12%)
  matrix products  35.1 us (12%)
  between operations  14.8 us (5%)
  local copies, waits for them, and re-layouts  14.1 us (5%)
  other arithmetic  10.5 us (3%)
  starting transfers between devices  4.93 us (2%)
    reduce_scatter x1, waiting for transfers between devices, per_device(): lax.psum_scatter(jnp.dot(hidden, down_matrix, preferred_element_type=jnp....  95.1 us
    all_gather x1, waiting for transfers between devices, per_device(): gathered = lax.all_gather(outbound, DP, axis=0, tiled=True)  92.4 us
    dot_general x1, matrix products, per_device(): jnp.dot(hidden, down_matrix, preferred_element_type=jnp.float32)  21.8 us
    all_to_all x1, blocking collectives, sum_at_owner(): tiles = lax.all_to_all(split_up(shard, dim, size), axis, 0, 0, tiled=True)  19.2 us
    psum x2, blocking collectives, over_axes(): shard = lax.psum(shard, axis)  16 us
    dot_general x1, matrix products, per_device(): jnp.dot(gathered, gate_matrix, preferred_element_type=jnp.float32)  12 us
    reduce_sum x1, other arithmetic, per_device(): weighted = jnp.sum(weights[:, :, None] * selected, axis=1)  8.66 us
  transfers between devices with their start and end apart: 3, of which 2 were waited for; matrix products, arithmetic and copies ran while one was open for 0% of the time, Pallas kernels for 0%

commit v1 on v0

--- a/solution.py
+++ b/solution.py
@@ -67,7 +67,9 @@
     targets, expert_loads = plan_routes(expert_ids, live_counts[0], n_experts, capacity)
     local_slots = targets - my_expert * capacity
     outbound = dispatch_rows(tokens, local_slots, capacity)
-    gathered = lax.all_gather(outbound, DP, axis=0, tiled=True)
+    gathered = jnp.concatenate(
+        lax.all_to_all(jnp.stack([outbound] * lax.axis_size(DP)), DP, 0, 0), axis=0
+    )
     gate_matrix = w_gate[0]
     up_matrix = w_up[0]
     down_matrix = w_down[0]

time: 303 us -> 363 us (1.20)
  blocking collectives: 35.2 us -> 184 us
  waiting for transfers between devices: 188 us -> 92.7 us
  local copies, waits for them, and re-layouts: 14.1 us -> 24.8 us
  matrix products: 35.1 us -> 30.8 us
    all_to_all x0 -> x1, blocking collectives: none -> 149 us  [per_device(): lax.all_to_all(jnp.stack([outbound] * lax.axis_size(DP)), DP, 0, 0)]
    all_gather x1 -> x0, waiting for transfers between devices: 92.4 us -> none  [per_device(): gathered = lax.all_gather(outbound, DP, axis=0, tiled=True)]
    another operation x1 -> x2, local copies, waits for them, and re-layouts: 0.01 us -> 6.17 us  [the longest x1 6.16 us: per_device(): jnp.stack([outbound] * lax.axis_size(DP))]
    unnamed x5 -> x11, local copies, waits for them, and re-layouts: 2.55 us -> 7.03 us
  transfers between devices with their start and end apart: 3 -> 2, of which waited for: 2 -> 1; matrix products, arithmetic and copies ran while one was open for 0% -> 0% of each run, Pallas kernels for 0% -> 0%
where the time goes in v1:
time: 363 us
  blocking collectives  184 us (51%)
  waiting for transfers between devices  92.7 us (26%)
  matrix products  30.8 us (8%)
  local copies, waits for them, and re-layouts  24.8 us (7%)
  between operations  14.8 us (4%)
  other arithmetic  10.5 us (3%)
  starting transfers between devices  4.89 us (1%)
    all_to_all x1, blocking collectives, per_device(): lax.all_to_all(jnp.stack([outbound] * lax.axis_size(DP)), DP, 0, 0)  149 us
    reduce_scatter x1, waiting for transfers between devices, per_device(): lax.psum_scatter(jnp.dot(hidden, down_matrix, preferred_element_type=jnp....  92.7 us
    dot_general x1, matrix products, per_device(): jnp.dot(hidden, down_matrix, preferred_element_type=jnp.float32)  21.8 us
    all_to_all x1, blocking collectives, sum_at_owner(): tiles = lax.all_to_all(split_up(shard, dim, size), axis, 0, 0, tiled=True)  19.3 us
    psum x2, blocking collectives, over_axes(): shard = lax.psum(shard, axis)  15.9 us
    reduce_sum x1, other arithmetic, per_device(): weighted = jnp.sum(weights[:, :, None] * selected, axis=1)  8.66 us
    dot_general x1, matrix products, per_device(): jnp.dot(gathered, gate_matrix, preferred_element_type=jnp.float32)  8.54 us
  transfers between devices with their start and end apart: 2, of which 1 were waited for; matrix products, arithmetic and copies ran while one was open for 0% of the time, Pallas kernels for 0%

profile of v1, /device:TPU:2, one launch (start us, length us, event | category | flops | bytes accessed | tf_op | source)
XLA Modules:
  0.0 362.8 jit_solution(15301409725315147975)
XLA Ops:
  7.2 0.0 copy-start
  7.2 0.0 reduce-scatter.2.cloned.1.call-start
  7.2 0.8 broadcast_multiply_fusion
  8.0 0.8 copy.17
  8.8 0.1 eq.43
  8.9 0.1 eq.39
  9.7 0.1 broadcast_in_dim.26
  9.8 0.1 broadcast_in_dim.27
  10.0 0.1 broadcast_in_dim.25
  10.1 0.1 and.20
  10.2 0.1 copy.19
  10.3 0.6 reduce-window.6
  10.9 0.2 slice_reduce_fusion
  11.2 0.1 convert_reduce_fusion
  11.3 0.1 reduce_sum.42
  11.5 0.8 copy.20
  12.3 0.1 fusion.15
  12.4 0.1 copy.21
  12.5 0.0 copy-done
  12.5 0.4 convolution_convert_fusion.1
  12.9 6.2 %stack.2 = bf16[16,96,4096]{2,1,0:T(8,128)(2,1)} broadcast(bf16[96,4096]{1,0:T(8,128)(2,1)S(1)} %convolution_convert_fusion.1), dimensions={1,2} | broadcast | bytes 13369344 | tf_op jit(solution)/shard_map/stack | solution.py:71
  19.0 0.0 copy-start.3
  19.0 149.1 %all_to_all.15 = bf16[16,96,4096]{2,1,0:T(8,128)(2,1)S(1)} all-to-all(bf16[16,96,4096]{2,1,0:T(8,128)(2,1)} %stack.2), channel_id=1, replica_groups=mesh['dp_0'=4,'dp_1'=4,'expert'=8] {'dp_0','dp_1'}, dimensions={0} | all-to-all | bytes 25165824 | tf_op jit(solution)/shard_map/all_to_all | solution.py:71
  168.1 0.0 copy-start.2
  168.1 4.5 %copy-done.2 = bf16[16,96,4096]{2,1,0:T(8,128)(2,1)} copy-done((bf16[16,96,4096]{2,1,0:T(8,128)(2,1)}, bf16[16,96,4096]{2,1,0:T(8,128)(2,1)S(1)}, u32[]{:S(2)}) %copy-start.2) | copy-done | bytes 12582936
  172.5 0.0 copy-done.3
  172.5 8.5 %fusion.3 = f32[1536,512]{1,0:T(8,128)} fusion(bf16[1536,4096]{1,0:T(8,128)(2,1)S(1)} %bitcast.29, bf16[1,4096,512]{2,1,0:T(8,128)(2,1)S(1)} %copy-done.3), kind=kOutput, calls=%fused_computation.6 | convolution fusion | flops 6442450944 | bytes 19922944 | tf_op jit(solution)/shard_map/dot_general | solution.py:76
  181.1 21.8 %convolution_convert_fusion = bf16[1536,4096]{1,0:T(8,128)(2,1)} fusion(bf16[1,512,4096]{2,1,0:T(8,128)(2,1)} %param.13, bf16[1536,4096]{1,0:T(8,128)(2,1)} %bitcast.30, bf16[1,4096,512]{2,1,0:T(8,128)(2,1)} %param.12, f32[1536,512]{1,0:T(8,128)} %fusion.3), kind=kOutput, calls=%fused_computation.1 | convolution fusion | flops 12895911936 | bytes 36700160 | tf_op jit(solution)/shard_map/dot_general | solution.py:80
  202.9 0.0 reduce-scatter.2.cloned.1.call-update
  203.0 0.1 reshape.61
  203.1 92.7 %reduce-scatter.2.cloned.1.call-done = bf16[96,4096]{1,0:T(8,128)(2,1)} async-done(((bf16[1536,4096]{1,0:T(8,128)(2,1)}), bf16[96,4096]{1,0:T(8,128)(2,1)}) %reduce-scatter.2.cloned.1.call-update) | async-done | bytes 786448 | tf_op jit(solution)/shard_map/reduce_scatter | solution.py:79
  295.8 5.1 %gather_fusion = bf16[256,4096]{1,0:T(8,128)(2,1)S(1)} fusion(bf16[96,4096]{1,0:T(8,128)(2,1)} %reduce-scatter.2.cloned.1.call-done, s32[1024]{0:T(1024)S(1)} %pad_clamp_fusion), kind=kCustom, calls=%fused_computation | custom fusion | bytes 4195328 | tf_op jit(solution)/shard_map/gather | solution.py:87
  300.9 4.0 %reshape.69 = f32[128,2,4096]{2,1,0:T(2,128)} reshape(bf16[256,4096]{1,0:T(8,128)(2,1)S(1)} %gather_fusion) | data formatting | bytes 6291456 | tf_op jit(solution)/shard_map/convert_element_type | solution.py:87
  304.9 8.7 %multiply_reduce_fusion = bf16[128,4096]{1,0:T(8,128)(2,1)S(1)} fusion(f32[128,2,4096]{2,1,0:T(2,128)} %reshape.69, f32[128,2]{1,0:T(8,128)S(1)} %get-tuple-element.4), kind=kLoop, calls=%fused_computation.8 | loop fusion | flops 1572864 | bytes 5243904 | tf_op jit(solution)/shard_map/reduce_sum | solution.py:89
  313.6 0.0 copy-start.1
  313.6 19.3 %all_to_all.16 = bf16[8,16,4096]{2,1,0:T(8,128)(2,1)S(1)} all-to-all(bf16[8,16,4096]{2,1,0:T(8,128)(2,1)S(1)} %bitcast.32), channel_id=1, replica_groups=mesh['dp_0'=4,'dp_1'=4,'expert'=8] {'expert'}, dimensions={0} | all-to-all | bytes 2097152 | tf_op jit(solution)/shard_map/all_to_all | solution.py:17
  332.9 0.1 reduce_sum.44
  333.1 1.1 broadcast_in_dim.31
  334.2 4.9 %all-to-all-start.2 = ((bf16[8,16,4096]{2,1,0:T(8,128)(2,1)}), bf16[8,16,4096]{2,1,0:T(8,128)(2,1)S(1)}, u32[]{:S(2)}, u32[]{:S(2)}) async-start(bf16[8,16,4096]{2,1,0:T(8,128)(2,1)} %broadcast_in_dim.31), calls=%async_computation.3 | async-start | bytes 2097152 | tf_op jit(solution)/shard_map/all_to_all | solution.py:23
  339.0 8.1 %psum.14 = s32[8]{0:T(128)S(1)} all-reduce(s32[8]{0:T(128)S(1)} %get-tuple-element.2), channel_id=1, replica_groups=mesh['dp_0'=4,'dp_1'=4,'expert'=8] {'dp_0'}, use_global_device_ids=true, to_apply=%region_8.9 | all-reduce | flops 8 | bytes 64 | tf_op jit(solution)/shard_map/psum | solution.py:39
  347.1 7.8 %psum.15 = s32[8]{0:T(128)} all-reduce(s32[8]{0:T(128)S(1)} %psum.14), channel_id=1, replica_groups=mesh['dp_0'=4,'dp_1'=4,'expert'=8] {'dp_1'}, use_global_device_ids=true, to_apply=%region_9.10 | all-reduce | flops 8 | bytes 64 | tf_op jit(solution)/shard_map/psum | solution.py:39
  355.0 0.0 all-to-all-done.2
  355.0 1.0 copy.25
  355.9 0.0 copy-done.1
  (8 shorter events, 0.1 us)
Async XLA Ops:
  7.2 5.3 %copy-start = (bf16[128,4096]{1,0:T(8,128)(2,1)S(1)}, bf16[128,4096]{1,0:T(8,128)(2,1)}, u32[]{:S(2)}) copy-start(bf16[128,4096]{1,0:T(8,128)(2,1)} %param.7) | copy-start | bytes 3145732
  7.2 288.6 %reduce-scatter.2.cloned.1.call-start = ((), (), s32[]{:S(2)}) async-start(), calls=%async_computation.4 | async-start | bytes 13369344 | tf_op jit(solution)/shard_map/reduce_scatter | solution.py:79
  19.0 153.5 %copy-start.3 = (bf16[1,4096,512]{2,1,0:T(8,128)(2,1)S(1)}, bf16[1,4096,512]{2,1,0:T(8,128)(2,1)}, u32[]{:S(2)}) copy-start(bf16[1,4096,512]{2,1,0:T(8,128)(2,1)} %param.11) | copy-start | bytes 12582916
  168.1 4.5 %copy-start.2 = (bf16[16,96,4096]{2,1,0:T(8,128)(2,1)}, bf16[16,96,4096]{2,1,0:T(8,128)(2,1)S(1)}, u32[]{:S(2)}) copy-start(bf16[16,96,4096]{2,1,0:T(8,128)(2,1)S(1)} %all_to_all.15) | copy-start | bytes 37748740
  313.6 42.3 %copy-start.1 = (bf16[128,4096]{1,0:T(8,128)(2,1)S(1)}, bf16[128,4096]{1,0:T(8,128)(2,1)}, u32[]{:S(2)}) copy-start(bf16[128,4096]{1,0:T(8,128)(2,1)} %param.7) | copy-start | bytes 3145732
  334.2 20.8 %all-to-all-start.2 = ((bf16[8,16,4096]{2,1,0:T(8,128)(2,1)}), bf16[8,16,4096]{2,1,0:T(8,128)(2,1)S(1)}, u32[]{:S(2)}, u32[]{:S(2)}) async-start(bf16[8,16,4096]{2,1,0:T(8,128)(2,1)} %broadcast_in_dim.31), calls=%async_computation.3 | async-start | bytes 2097152 | tf_op jit(solution)/shard_map/all_to_all | solution.py:23
Sparse Core Ops, SparseCore 0:
  203.1 92.6 reduce-scatter.1
